TPU v7x, 32 devices: a whole 2x2x4 slice. The times are simulated.
32 devices in a mesh: layer: 4 (over y, core), slab: 8 (over z, x).
Axes of the slice: x: 2, y: 2, z: 4, core: 2. Of those that a mesh axis runs over, the one named last changes fastest.
Arguments:
- weights: bfloat16 [8192, 16384], P('slab', 'layer'), may hold values from -0.29882812 to 0.29882812
- whitening: bfloat16 [8192, 8192], P('slab'), may hold values from -1 to 10, as said below
- test_matrix: int32 [16384, 1024], P(('layer', 'slab')), may hold values from -4 to 4
Outputs:
- basis: float32 [8192, 1024], P('slab')
- coefficients: float32 [16384, 1024], P('layer', 'slab')
Inputs may be any that keep to these rules, and one draw needn't show every extreme that they name: whitening is lower triangular with diagonal entries between 1 and 10.
All inputs are finite; a program needn't handle non-finite values.
Results may differ from a plain program's by a relative error of at most 0.006.
Values may be sent and summed in bfloat16 or wider, within the bound.
A program may use at most 128 MiB of HBM per device.

v0:
```python
import math
import jax
import jax.numpy as jnp
from jax import lax
from jax.sharding import PartitionSpec as P

D = 8192


def on_device(weights, whitening, test_matrix):
    rank_width = test_matrix.shape[1]
    slice_width = rank_width // lax.axis_size("layer")
    test_values = test_matrix.astype(jnp.bfloat16)
    columns = weights
    sketch_terms = jnp.dot(
        columns,
        lax.all_gather(test_values, "slab", axis=0, tiled=True),
        preferred_element_type=jnp.float32,
    )
    sketch = lax.psum_scatter(sketch_terms, "layer", scatter_dimension=1, tiled=True).astype(
        jnp.bfloat16
    )
    columns = whitening
    whitened_part = jnp.dot(
        columns,
        lax.all_gather(sketch, "slab", axis=0, tiled=True),
        preferred_element_type=jnp.float32,
    )
    whitened = lax.all_gather(whitened_part, "layer", axis=1, tiled=True)
    local_gram = jnp.dot(
        whitened.T, whitened, precision=lax.Precision.HIGHEST, preferred_element_type=jnp.float32
    )
    gram_matrix = lax.psum(local_gram, "slab")
    factor = jnp.linalg.cholesky(gram_matrix)
    ortho = jax.scipy.linalg.solve_triangular(factor, whitened.T, lower=True).T
    basis_half = ortho.astype(jnp.bfloat16)
    basis = basis_half.astype(jnp.float32) * math.sqrt(D)
    own_slice = lax.dynamic_slice_in_dim(
        basis_half, lax.axis_index("layer") * slice_width, slice_width, 1
    )
    columns = whitening
    projected_part = lax.psum_scatter(
        lax.dot_general(
            columns, own_slice, (((0,), (0,)), ((), ())), preferred_element_type=jnp.float32
        ),
        "slab",
        scatter_dimension=0,
        tiled=True,
    ).astype(jnp.bfloat16)
    projected = lax.all_gather(projected_part, "layer", axis=1, tiled=True)
    columns = weights
    coefficients = lax.psum_scatter(
        lax.dot_general(
            columns, projected, (((0,), (0,)), ((), ())), preferred_element_type=jnp.float32
        ),
        "slab",
        scatter_dimension=1,
        tiled=True,
    )
    return (basis, coefficients)


def solution(mesh):
    placed = (P("slab", "layer"), P("slab", None), P(("layer", "slab"), None))
    return jax.shard_map(
        on_device,
        mesh=mesh,
        in_specs=placed,
        out_specs=(P("slab", None), P("layer", "slab")),
        check_vma=False,
    )
```

profile of v0, /device:TPU:0, one launch (start us, length us, event | category | flops | bytes accessed | tf_op | source)
XLA Modules:
  0.0 1321.0 jit_solution(4433787939744664165)
XLA Ops:
  7.2 2.8 convert_element_type.15
  10.1 127.8 %all-gather.5.cloned.1.call-done = bf16[4096,1024]{1,0:T(8,128)(2,1)} async-done(((bf16[512,1024]{1,0:T(8,128)(2,1)}), bf16[4096,1024]{1,0:T(8,128)(2,1)}) %all-gather.5.cloned.1.call-update) | async-done | bytes 8388624 | tf_op jit(solution)/shard_map/all_gather | solution.py:17
  137.9 14.9 %fusion.73 = f32[1024,1024]{1,0:T(8,128)} fusion(bf16[1024,4096]{1,0:T(8,128)(2,1)} %param.3, bf16[4096,1024]{1,0:T(8,128)(2,1)} %all-gather.5.cloned.1.call-done), kind=kOutput, calls=%fused_computation.164 | convolution fusion | flops 8589934592 | bytes 20971520 | tf_op jit(solution)/shard_map/dot_general | solution.py:15
  152.9 42.7 %reduce-scatter.4.cloned.1.call-done = f32[1024,256]{1,0:T(8,128)} async-done(((f32[1024,1024]{1,0:T(8,128)}), f32[1024,256]{1,0:T(8,128)}) %reduce-scatter.4.cloned.1.call-update) | async-done | bytes 1048592 | tf_op jit(solution)/shard_map/reduce_scatter | solution.py:20
  197.8 73.4 %all-gather.7.cloned.1.call-done = bf16[8192,256]{1,0:T(8,128)(2,1)} async-done(((bf16[1024,256]{1,0:T(8,128)(2,1)}), bf16[8192,256]{1,0:T(8,128)(2,1)}) %all-gather.7.cloned.1.call-update) | async-done | bytes 4194320 | tf_op jit(solution)/shard_map/all_gather | solution.py:26
  271.1 12.6 convolution_bitcast_fusion.2
  284.0 32.9 %all-gather.9.cloned.1.call-done = f32[1024,1024]{0,1:T(8,128)} async-done(((f32[1024,256]{0,1:T(8,128)}), f32[1024,1024]{0,1:T(8,128)}) %all-gather.9.cloned.1.call-update) | async-done | bytes 4194320 | tf_op jit(solution)/shard_map/all_gather | solution.py:29
  316.9 18.2 %fusion.74 = f32[1024,1024]{0,1:T(8,128)} fusion(f32[1024,1024]{0,1:T(8,128)} %all-gather.9.cloned.1.call-done), kind=kOutput, calls=%fused_computation.165 | convolution fusion | flops 12884901888 | bytes 8388608 | tf_op jit(solution)/shard_map/dot_general | solution.py:30
  335.2 156.5 %all-reduce.3.cloned.1.call-done = f32[1024,1024]{0,1:T(8,128)} async-done(((f32[1024,1024]{0,1:T(8,128)}), f32[1024,1024]{0,1:T(8,128)}) %all-reduce.3.cloned.1.call-update) | async-done | bytes 4194320 | tf_op jit(solution)/shard_map/psum | solution.py:33
  491.6 5.7 copy.6
  497.4 4.4 fusion
  503.8 11.7 cholesky.223
  515.5 9.8 custom-call.63
  525.4 2.5 cholesky.255
  527.9 2.3 constant_dynamic-update-slice_fusion.25
  531.8 11.9 cholesky.244
  544.3 9.8 custom-call.64
  557.4 11.7 cholesky.468
  570.4 9.8 custom-call.65
  581.3 2.3 convolution_subtract_fusion.7
  583.7 11.9 cholesky.487
  596.9 9.8 custom-call.66
  607.8 2.3 convolution_subtract_fusion.8
  610.1 11.7 cholesky.506
  623.1 10.2 custom-call.67
  634.3 2.3 convolution_subtract_fusion.9
  636.6 11.7 cholesky.526
  649.6 9.8 custom-call.68
  662.4 11.9 cholesky.546
  675.5 9.8 custom-call.69
  688.0 11.7 cholesky.564
  706.5 4.9 select_select_fusion
  711.4 22.8 %while.1 = (s32[]{:T(128)}, f32[1024,1024]{1,0:T(8,128)}, s32[8,2]{0,1:T(2,128)S(1)}, f32[8,128,128]{2,1,0:T(8,128)S(1)}, s32[]{:T(128)}) while((s32[]{:T(128)}, f32[1024,1024]{1,0:T(8,128)}, s32[8,2]{0,1:T(2,128)S(1)}, f32[8,128,128]{2,1,0:T(8,128)S(1)}, s32[]{:T(128)}) %tuple.58), condition=%wide.while_cond, body=%wide.while_body.sunk | while | flops 2 | bytes 131181 | solution.py:35
  714.9 2.2 bitcast_dynamic-update-slice_fusion.2
  720.6 2.2 bitcast_dynamic-update-slice_fusion.2
  734.2 78.8 %custom-call.70 = f32[8,128,128]{1,2,0:T(8,128)S(1)} custom-call(f32[8,128,128]{2,1,0:T(8,128)S(1)} %get-tuple-element.9), custom_call_target="InvertDiagBlocksLowerTriangular" | custom-call | tf_op jit(solution)/shard_map/jit(_solve_triangular)/triangular_solve | solution.py:35
  822.3 2.4 fusion.18
  826.0 2.9 convolution_subtract_fusion.2
  829.7 3.0 convolution_subtract_fusion.1
  833.4 3.5 convolution_subtract_fusion.3
  837.6 6.7 convolution_bitcast_fusion
  844.3 147.0 %reduce-scatter.6.cloned.1.call-done = f32[1024,256]{0,1:T(8,128)} async-done(((f32[8192,256]{0,1:T(8,128)}), f32[1024,256]{0,1:T(8,128)}) %reduce-scatter.6.cloned.1.call-update) | async-done | bytes 1048592 | tf_op jit(solution)/shard_map/reduce_scatter | solution.py:42
  993.5 21.8 %all-gather.11.cloned.1.call-done = bf16[1024,1024]{0,1:T(8,128)(2,1)} async-done(((bf16[1024,256]{0,1:T(8,128)(2,1)}), bf16[1024,1024]{0,1:T(8,128)(2,1)}) %all-gather.11.cloned.1.call-update) | async-done | bytes 2097168 | tf_op jit(solution)/shard_map/all_gather | solution.py:50
  1015.2 16.0 %convolution_bitcast_fusion.1 = f32[4096,1024]{0,1:T(8,128)} fusion(bf16[1024,1024]{0,1:T(8,128)(2,1)} %all-gather.11.cloned.1.call-done, bf16[1024,4096]{1,0:T(8,128)(2,1)} %param.3), kind=kOutput, calls=%fused_computation.3 | convolution fusion | flops 8589934592 | bytes 27262976 | tf_op jit(solution)/shard_map/dot_general | solution.py:53
  1031.2 2.5 multiply_bitcast_fusion
  1033.7 5.3 copy.7
  1039.1 271.7 %reduce-scatter.8.cloned.1.call-done = f32[4096,128]{0,1:T(8,128)} async-done(((f32[4096,1024]{0,1:T(8,128)}), f32[4096,128]{0,1:T(8,128)}) %reduce-scatter.8.cloned.1.call-update) | async-done | bytes 2097168 | tf_op jit(solution)/shard_map/reduce_scatter | solution.py:52
  1310.8 2.9 copy.8
  (106 shorter events, 60.3 us)
Async XLA Ops:
  7.2 130.7 %all-gather.5.cloned.1.call-start = ((), (), s32[]{:S(2)}) async-start(), calls=%async_computation.3 | async-start | bytes 9437184 | tf_op jit(solution)/shard_map/all_gather | solution.py:17
  10.0 185.6 %reduce-scatter.4.cloned.1.call-start = ((), (), s32[]{:S(2)}) async-start(), calls=%async_computation.4 | async-start | bytes 5242880 | tf_op jit(solution)/shard_map/reduce_scatter | solution.py:20
  152.9 118.3 %all-gather.7.cloned.1.call-start = ((), (), s32[]{:S(2)}) async-start(), calls=%async_computation.5 | async-start | bytes 4718592 | tf_op jit(solution)/shard_map/all_gather | solution.py:26
  197.7 119.2 %all-gather.9.cloned.1.call-start = ((), (), s32[]{:S(2)}) async-start(), calls=%async_computation.6 | async-start | bytes 5242880 | tf_op jit(solution)/shard_map/all_gather | solution.py:29
  283.7 207.9 %all-reduce.3.cloned.1.call-start = ((), (), s32[]{:S(2)}) async-start(), calls=%async_computation.7 | async-start | bytes 8388608 | tf_op jit(solution)/shard_map/psum | solution.py:33
  335.1 656.2 %reduce-scatter.6.cloned.1.call-start = ((), (), s32[]{:S(2)}) async-start(), calls=%async_computation.8 | async-start | bytes 9437184 | tf_op jit(solution)/shard_map/reduce_scatter | solution.py:42
  501.8 2.0 copy-start
  813.1 4.3 copy-start.1
  822.3 15.2 %slice-start = ((s8[16777216]{0:T(1024)(128)(4,1)}), s8[4194304]{0:T(1024)(128)(4,1)S(1)}, s32[]{:S(2)}) async-start(s8[16777216]{0:T(1024)(128)(4,1)} %bitcast.119), calls=%async_computation.11 | async-start | bytes 8388608
  825.5 12.0 slice-start.1
  826.0 11.6 slice-start.2
  829.7 7.9 slice-start.3
  844.3 171.0 %all-gather.11.cloned.1.call-start = ((), (), s32[]{:S(2)}) async-start(), calls=%async_computation.9 | async-start | bytes 2621440 | tf_op jit(solution)/shard_map/all_gather | solution.py:50
  993.4 317.4 %reduce-scatter.8.cloned.1.call-start = ((), (), s32[]{:S(2)}) async-start(), calls=%async_computation.10 | async-start | bytes 18874368 | tf_op jit(solution)/shard_map/reduce_scatter | solution.py:52
Sparse Core Ops, SparseCore 0:
  10.7 127.1 all-gather.4
  153.0 42.5 reduce-scatter.3
  198.3 72.7 all-gather.6
  283.9 32.9 all-gather.8
  335.2 156.3 all-reduce.2
  844.4 146.8 reduce-scatter.5
  993.5 21.6 all-gather.10
  1031.3 279.4 reduce-scatter.7
where the time goes:
time: 1330 us; the launch traced here: 1320 us
  waiting for transfers between devices  874 us (66%)
  other arithmetic  270 us (20%)
  matrix products  115 us (9%)
  local copies, waits for them, and re-layouts  42.1 us (3%)
  between operations  19.9 us (1%)
    reduce_scatter x1, waiting for transfers between devices, on_device(): lax.psum_scatter(lax.dot_general(columns, projected, (((0,), (0,)), ((),...  272 us
    another operation x30, other arithmetic, on_device(): factor = jnp.linalg.cholesky(gram_matrix)  172 us
    psum x1, waiting for transfers between devices, on_device(): gram_matrix = lax.psum(local_gram, 'slab')  156 us
    reduce_scatter x1, waiting for transfers between devices, on_device(): lax.psum_scatter(lax.dot_general(columns, own_slice, (((0,), (0,)), ((),...  147 us
    all_gather x1, waiting for transfers between devices, on_device(): lax.all_gather(test_values, 'slab', axis=0, tiled=True)  128 us
    another operation x3, other arithmetic, on_device(): ortho = jax.scipy.linalg.solve_triangular(factor, whitened.T, lower=True).T  83.7 us
    all_gather x1, waiting for transfers between devices, on_device(): lax.all_gather(sketch, 'slab', axis=0, tiled=True)  73.4 us
    reduce_scatter x1, waiting for transfers between devices, on_device(): lax.psum_scatter(sketch_terms, 'layer', scatter_dimension=1, tiled=True)  42.7 us
  transfers between devices with their start and end apart: 8, of which 8 were waited for; matrix products, arithmetic and copies ran while one was open for 1% of the time, Pallas kernels for 0%

commit v1 on v0

--- a/solution.py
+++ b/solution.py
@@ -5,6 +5,13 @@
 from jax.sharding import PartitionSpec as P
 
 D = 8192
+
+
+def exchange_gather(x, axis, dim):
+    size = lax.axis_size(axis)
+    blocks = jnp.stack([x for _ in range(size)])
+    blocks = lax.all_to_all(blocks, axis, split_axis=0, concat_axis=0)
+    return jnp.concatenate(blocks, axis=dim)
 
 
 def on_device(weights, whitening, test_matrix):
@@ -22,9 +29,7 @@
     )
     columns = whitening
     whitened_part = jnp.dot(
-        columns,
-        lax.all_gather(sketch, "slab", axis=0, tiled=True),
-        preferred_element_type=jnp.float32,
+        columns, exchange_gather(sketch, "slab", 0), preferred_element_type=jnp.float32
     )
     whitened = lax.all_gather(whitened_part, "layer", axis=1, tiled=True)
     local_gram = jnp.dot(

time: 1330 us -> 1350 us (1.015)
  blocking collectives: 0 us -> 98.4 us
  waiting for transfers between devices: 874 us -> 800 us
    all_to_all x0 -> x1, blocking collectives: none -> 98.4 us  [exchange_gather(): blocks = lax.all_to_all(blocks, axis, split_axis=0, concat_axis=0)]
    all_gather x1 -> x0, waiting for transfers between devices: 73.4 us -> none  [on_device(): lax.all_gather(sketch, 'slab', axis=0, tiled=True)]
  transfers between devices with their start and end apart: 8 -> 7, of which waited for: 8 -> 7; matrix products, arithmetic and copies ran while one was open for 1% -> 1% of each run, Pallas kernels for 0% -> 0%
where the time goes in v1:
time: 1350 us; the launch traced here: 1340 us
  waiting for transfers between devices  800 us (59%)
  other arithmetic  269 us (20%)
  matrix products  115 us (9%)
  blocking collectives  98.4 us (7%)
  local copies, waits for them, and re-layouts  42.4 us (3%)
  between operations  19.9 us (1%)
    reduce_scatter x1, waiting for transfers between devices, on_device(): lax.psum_scatter(lax.dot_general(columns, projected, (((0,), (0,)), ((),...  272 us
    another operation x30, other arithmetic, on_device(): factor = jnp.linalg.cholesky(gram_matrix)  172 us
    psum x1, waiting for transfers between devices, on_device(): gram_matrix = lax.psum(local_gram, 'slab')  156 us
    reduce_scatter x1, waiting for transfers between devices, on_device(): lax.psum_scatter(lax.dot_general(columns, own_slice, (((0,), (0,)), ((),...  147 us
    all_gather x1, waiting for transfers between devices, on_device(): lax.all_gather(test_values, 'slab', axis=0, tiled=True)  128 us
    all_to_all x1, blocking collectives, exchange_gather(): blocks = lax.all_to_all(blocks, axis, split_axis=0, concat_axis=0)  98.4 us
    another operation x3, other arithmetic, on_device(): ortho = jax.scipy.linalg.solve_triangular(factor, whitened.T, lower=True).T  83.7 us
    reduce_scatter x1, waiting for transfers between devices, on_device(): lax.psum_scatter(sketch_terms, 'layer', scatter_dimension=1, tiled=True)  42.7 us
  transfers between devices with their start and end apart: 7, of which 7 were waited for; matrix products, arithmetic and copies ran while one was open for 1% of the time, Pallas kernels for 0%

profile of v1, /device:TPU:0, one launch (start us, length us, event | category | flops | bytes accessed | tf_op | source)
XLA Modules:
  0.0 1345.0 jit_solution(10391996027569151313)
XLA Ops:
  7.2 2.8 convert_element_type.15
  10.1 127.8 %all-gather.4.cloned.1.call-done = bf16[4096,1024]{1,0:T(8,128)(2,1)} async-done(((bf16[512,1024]{1,0:T(8,128)(2,1)}), bf16[4096,1024]{1,0:T(8,128)(2,1)}) %all-gather.4.cloned.1.call-update) | async-done | bytes 8388624 | tf_op jit(solution)/shard_map/all_gather | solution.py:24
  137.9 14.9 %fusion.73 = f32[1024,1024]{1,0:T(8,128)} fusion(bf16[1024,4096]{1,0:T(8,128)(2,1)} %param.3, bf16[4096,1024]{1,0:T(8,128)(2,1)} %all-gather.4.cloned.1.call-done), kind=kOutput, calls=%fused_computation.164 | convolution fusion | flops 8589934592 | bytes 20971520 | tf_op jit(solution)/shard_map/dot_general | solution.py:22
  152.9 42.7 %reduce-scatter.4.cloned.1.call-done = f32[1024,256]{1,0:T(8,128)} async-done(((f32[1024,1024]{1,0:T(8,128)}), f32[1024,256]{1,0:T(8,128)}) %reduce-scatter.4.cloned.1.call-update) | async-done | bytes 1048592 | tf_op jit(solution)/shard_map/reduce_scatter | solution.py:27
  197.2 98.4 %all_to_all.5 = bf16[8,1024,256]{2,1,0:T(8,128)(2,1)} all-to-all(bf16[8,1024,256]{2,1,0:T(8,128)(2,1)S(1)} %stack.2), channel_id=1, replica_groups=mesh['layer'=4,'slab'=8] {'slab'}, dimensions={0} | all-to-all | bytes 8388608 | tf_op jit(solution)/shard_map/all_to_all | solution.py:13
  295.6 12.6 convolution_bitcast_fusion.2
  308.5 32.4 %all-gather.6.cloned.1.call-done = f32[1024,1024]{0,1:T(8,128)} async-done(((f32[1024,256]{0,1:T(8,128)}), f32[1024,1024]{0,1:T(8,128)}) %all-gather.6.cloned.1.call-update) | async-done | bytes 4194320 | tf_op jit(solution)/shard_map/all_gather | solution.py:34
  340.9 18.2 %fusion.74 = f32[1024,1024]{0,1:T(8,128)} fusion(f32[1024,1024]{0,1:T(8,128)} %all-gather.6.cloned.1.call-done), kind=kOutput, calls=%fused_computation.165 | convolution fusion | flops 12884901888 | bytes 8388608 | tf_op jit(solution)/shard_map/dot_general | solution.py:35
  359.2 156.5 %all-reduce.3.cloned.1.call-done = f32[1024,1024]{0,1:T(8,128)} async-done(((f32[1024,1024]{0,1:T(8,128)}), f32[1024,1024]{0,1:T(8,128)}) %all-reduce.3.cloned.1.call-update) | async-done | bytes 4194320 | tf_op jit(solution)/shard_map/psum | solution.py:38
  515.6 5.7 copy.6
  521.4 4.4 fusion
  527.8 11.7 cholesky.223
  539.5 9.8 custom-call.63
  549.4 2.5 cholesky.255
  551.9 2.3 constant_dynamic-update-slice_fusion.25
  555.8 11.9 cholesky.244
  568.3 9.8 custom-call.64
  581.4 11.7 cholesky.468
  594.4 9.8 custom-call.65
  605.3 2.3 convolution_subtract_fusion.7
  607.7 11.9 cholesky.487
  620.9 9.8 custom-call.66
  631.7 2.3 convolution_subtract_fusion.8
  634.1 11.7 cholesky.506
  647.1 10.2 custom-call.67
  658.3 2.3 convolution_subtract_fusion.9
  660.6 11.7 cholesky.526
  673.6 9.8 custom-call.68
  686.4 11.9 cholesky.546
  699.5 9.8 custom-call.69
  711.9 11.7 cholesky.564
  730.5 4.9 select_select_fusion
  735.4 22.8 %while.1 = (s32[]{:T(128)}, f32[1024,1024]{1,0:T(8,128)}, s32[8,2]{0,1:T(2,128)S(1)}, f32[8,128,128]{2,1,0:T(8,128)S(1)}, s32[]{:T(128)}) while((s32[]{:T(128)}, f32[1024,1024]{1,0:T(8,128)}, s32[8,2]{0,1:T(2,128)S(1)}, f32[8,128,128]{2,1,0:T(8,128)S(1)}, s32[]{:T(128)}) %tuple.58), condition=%wide.while_cond, body=%wide.while_body.sunk | while | flops 2 | bytes 131181 | solution.py:40
  738.9 2.2 bitcast_dynamic-update-slice_fusion.2
  744.6 2.2 bitcast_dynamic-update-slice_fusion.2
  758.2 78.8 %custom-call.70 = f32[8,128,128]{1,2,0:T(8,128)S(1)} custom-call(f32[8,128,128]{2,1,0:T(8,128)S(1)} %get-tuple-element.9), custom_call_target="InvertDiagBlocksLowerTriangular" | custom-call | tf_op jit(solution)/shard_map/jit(_solve_triangular)/triangular_solve | solution.py:40
  846.3 2.4 fusion.18
  850.0 2.9 convolution_subtract_fusion.2
  853.7 3.0 convolution_subtract_fusion.1
  857.4 3.5 convolution_subtract_fusion.3
  861.6 6.7 convolution_bitcast_fusion
  868.3 147.0 %reduce-scatter.6.cloned.1.call-done = f32[1024,256]{0,1:T(8,128)} async-done(((f32[8192,256]{0,1:T(8,128)}), f32[1024,256]{0,1:T(8,128)}) %reduce-scatter.6.cloned.1.call-update) | async-done | bytes 1048592 | tf_op jit(solution)/shard_map/reduce_scatter | solution.py:47
  1017.4 21.8 %all-gather.8.cloned.1.call-done = bf16[1024,1024]{0,1:T(8,128)(2,1)} async-done(((bf16[1024,256]{0,1:T(8,128)(2,1)}), bf16[1024,1024]{0,1:T(8,128)(2,1)}) %all-gather.8.cloned.1.call-update) | async-done | bytes 2097168 | tf_op jit(solution)/shard_map/all_gather | solution.py:55
  1039.2 16.0 %convolution_bitcast_fusion.1 = f32[4096,1024]{0,1:T(8,128)} fusion(bf16[1024,1024]{0,1:T(8,128)(2,1)} %all-gather.8.cloned.1.call-done, bf16[1024,4096]{1,0:T(8,128)(2,1)} %param.3), kind=kOutput, calls=%fused_computation.3 | convolution fusion | flops 8589934592 | bytes 27262976 | tf_op jit(solution)/shard_map/dot_general | solution.py:58
  1055.2 2.5 multiply_bitcast_fusion
  1057.7 5.3 copy.7
  1063.1 271.7 %reduce-scatter.8.cloned.1.call-done = f32[4096,128]{0,1:T(8,128)} async-done(((f32[4096,1024]{0,1:T(8,128)}), f32[4096,128]{0,1:T(8,128)}) %reduce-scatter.8.cloned.1.call-update) | async-done | bytes 2097168 | tf_op jit(solution)/shard_map/reduce_scatter | solution.py:57
  1334.8 2.9 copy.8
  (105 shorter events, 59.7 us)
Async XLA Ops:
  7.2 130.7 %all-gather.4.cloned.1.call-start = ((), (), s32[]{:S(2)}) async-start(), calls=%async_computation.4 | async-start | bytes 9437184 | tf_op jit(solution)/shard_map/all_gather | solution.py:24
  10.0 185.6 %reduce-scatter.4.cloned.1.call-start = ((), (), s32[]{:S(2)}) async-start(), calls=%async_computation.5 | async-start | bytes 5242880 | tf_op jit(solution)/shard_map/reduce_scatter | solution.py:27
  152.9 188.0 %all-gather.6.cloned.1.call-start = ((), (), s32[]{:S(2)}) async-start(), calls=%async_computation.6 | async-start | bytes 5242880 | tf_op jit(solution)/shard_map/all_gather | solution.py:34
  308.2 207.4 %all-reduce.3.cloned.1.call-start = ((), (), s32[]{:S(2)}) async-start(), calls=%async_computation.7 | async-start | bytes 8388608 | tf_op jit(solution)/shard_map/psum | solution.py:38
  359.1 656.2 %reduce-scatter.6.cloned.1.call-start = ((), (), s32[]{:S(2)}) async-start(), calls=%async_computation.8 | async-start | bytes 9437184 | tf_op jit(solution)/shard_map/reduce_scatter | solution.py:47
  525.8 2.0 copy-start
  837.0 4.3 copy-start.1
  846.3 15.2 %slice-start = ((s8[16777216]{0:T(1024)(128)(4,1)}), s8[4194304]{0:T(1024)(128)(4,1)S(1)}, s32[]{:S(2)}) async-start(s8[16777216]{0:T(1024)(128)(4,1)} %bitcast.120), calls=%async_computation.11 | async-start | bytes 8388608
  849.5 12.0 slice-start.1
  850.0 11.6 slice-start.2
  853.6 7.9 slice-start.3
  868.3 171.0 %all-gather.8.cloned.1.call-start = ((), (), s32[]{:S(2)}) async-start(), calls=%async_computation.9 | async-start | bytes 2621440 | tf_op jit(solution)/shard_map/all_gather | solution.py:55
  1017.4 317.4 %reduce-scatter.8.cloned.1.call-start = ((), (), s32[]{:S(2)}) async-start(), calls=%async_computation.10 | async-start | bytes 18874368 | tf_op jit(solution)/shard_map/reduce_scatter | solution.py:57
Sparse Core Ops, SparseCore 0:
  10.7 127.1 all-gather.3
  153.0 42.5 reduce-scatter.3
  308.3 32.5 all-gather.5
  359.2 156.3 all-reduce.2
  868.4 146.8 reduce-scatter.5
  1017.5 21.6 all-gather.7
  1055.3 279.4 reduce-scatter.7
